TPU v7x, 32 devices: a whole 2x2x4 slice. The times are simulated.
32 devices in a mesh: dp: 8 (over y, x, core), pipe: 4 (over z).
Axes of the slice: x: 2, y: 2, z: 4, core: 2. Of those that a mesh axis runs over, the one named last changes fastest.
Arguments:
- embed_grad: bfloat16 [512, 4608], P('dp', 'pipe'), may hold values from -0.35 to 0.35
- ids: int32 [512], P('dp'), may hold values from 0 to 11263
Outputs:
- table_grad: float32 [11264, 4608], P('dp', 'pipe')
All inputs are finite; a program needn't handle non-finite values.
Results may differ from a plain program's by a relative error of at most 0.00035.
Values may be sent and summed in bfloat16 or wider, within the bound.
A program may use at most 64 MiB of HBM per device.

v0:
```python
import math

import jax
import jax.numpy as jnp
from jax import lax
from jax.sharding import PartitionSpec as P

D = 4608
VOC_DEV = 1408


def segment_rows(cotangent, token_ids, offset):
    local = token_ids - offset
    inside = (local >= 0) & (local < VOC_DEV)
    segment = jnp.where(inside, local, VOC_DEV).astype(jnp.int32)
    summed = jax.ops.segment_sum(cotangent.astype(jnp.float32), segment, VOC_DEV + 1)
    return summed[:VOC_DEV]


def per_device(embed_grad, ids):
    offset = lax.axis_index("dp") * VOC_DEV
    cotangent_all, ids_all = (
        lax.all_gather(embed_grad, "dp", axis=0, tiled=True),
        lax.all_gather(ids, "dp", axis=0, tiled=True),
    )
    summed = segment_rows(cotangent_all, ids_all, offset)
    grad_rows = summed * math.sqrt(D)
    total = lax.psum(jnp.sum(grad_rows * grad_rows), ("dp", "pipe"))
    grad_norm = jnp.sqrt(total + 1e-06)
    tokens_all = embed_grad.shape[0] * lax.axis_size("dp")
    factor = jnp.minimum(1.0, 0.2 * math.sqrt(tokens_all * D) / grad_norm)
    return grad_rows * factor


def solution(mesh):
    placed = (P("dp", "pipe"), P("dp"))
    return jax.shard_map(
        per_device, mesh=mesh, in_specs=placed, out_specs=P("dp", "pipe"), check_vma=False
    )
```

profile of v0, /device:TPU:0, one launch (start us, length us, event | category | flops | bytes accessed | tf_op | source)
XLA Modules:
  0.0 103.2 jit_solution(16270416561450067382)
XLA Ops:
  6.5 0.0 all-gather.2.cloned.1.call-start
  6.5 0.7 all-gather.2.cloned.1.call-update
  7.3 1.2 %dynamic-slice = u32[1]{0:T(128)} dynamic-slice(u32[32]{0:T(128)} %constant.24, u32[]{:T(128)S(6)} %add.8), dynamic_slice_sizes={1} | dynamic-slice | bytes 12
  9.2 0.9 dynamic-update-slice
  10.0 9.5 %all-reduce = s32[512]{0:T(512)S(1)} all-reduce(s32[512]{0:T(512)S(1)} %dynamic-update-slice), channel_id=1, replica_groups=mesh['dp'=8,'pipe'=4] {'dp'}, use_global_device_ids=true, to_apply=%add | all-reduce | flops 512 | bytes 4096
  19.5 16.4 %all-gather.2.cloned.1.call-done = bf16[512,1152]{1,0:T(8,128)(2,1)} async-done(((bf16[64,1152]{1,0:T(8,128)(2,1)}), bf16[512,1152]{1,0:T(8,128)(2,1)}) %all-gather.2.cloned.1.call-update) | async-done | bytes 1179664 | tf_op jit(solution)/shard_map/all_gather | solution.py:23
  35.9 9.1 %scatter_custom_fusion = f32[1409,1152]{1,0:T(8,128)} fusion(s32[512]{0:T(512)S(1)} %and_select_fusion, f32[]{:T(128)} %constant.9.clone.1, bf16[512,1152]{1,0:T(8,128)(2,1)} %all-gather.2.cloned.1.call-done), kind=kCustom, calls=%fused_computation.3 | custom fusion | flops 1179648 | bytes 7672324 | tf_op jit(solution)/shard_map/scatter-add | solution.py:16
  45.0 5.1 %multiply_reduce_fusion = f32[]{:T(128)} fusion(f32[1409,1152]{1,0:T(8,128)} %scatter_custom_fusion), kind=kLoop, calls=%fused_computation.1 | loop fusion | flops 4866047 | bytes 6488068 | tf_op jit(solution)/shard_map/reduce_sum | solution.py:28
  50.2 39.5 %psum.7 = f32[]{:T(128)} all-reduce(f32[]{:T(128)} %multiply_reduce_fusion), channel_id=1, replica_groups=mesh['dp'=8,'pipe'=4] {'dp','pipe'}, use_global_device_ids=true, to_apply=%region_2.3 | all-reduce | flops 1 | bytes 8 | tf_op jit(solution)/shard_map/psum | solution.py:28
  90.3 6.0 %slice_multiply_fusion = f32[1408,1152]{1,0:T(8,128)} fusion(f32[1409,1152]{1,0:T(8,128)} %scatter_custom_fusion, f32[]{:T(128)S(6)} %mul.24), kind=kLoop, calls=%fused_computation.2 | loop fusion | flops 1622016 | bytes 12976132 | tf_op jit(solution)/shard_map/mul | solution.py:32
  (2 shorter events, 0.0 us)
Async XLA Ops:
  6.5 29.4 %all-gather.2.cloned.1.call-start = ((), (), s32[]{:S(2)}) async-start(), calls=%async_computation | async-start | bytes 1327104 | tf_op jit(solution)/shard_map/all_gather | solution.py:23
Sparse Core Ops, SparseCore 0:
  9.2 26.6 all-gather.1
where the time goes:
time: 104 us; the launch traced here: 103 us
  blocking collectives  49 us (47%)
  other arithmetic  20.3 us (20%)
  waiting for transfers between devices  17.1 us (16%)
  between operations  14.8 us (14%)
  local copies, waits for them, and re-layouts  2.1 us (2%)
    psum x1, blocking collectives, per_device(): total = lax.psum(jnp.sum(grad_rows * grad_rows), ('dp', 'pipe'))  39.5 us
    all_gather x1, waiting for transfers between devices, per_device(): lax.all_gather(embed_grad, 'dp', axis=0, tiled=True)  16.4 us
    unnamed x1, blocking collectives  9.49 us
    scatter-add x1, other arithmetic, segment_rows(): jax.ops.segment_sum(cotangent.astype(jnp.float32), segment, VOC_DEV + 1)  9.15 us
    mul x1, other arithmetic, per_device(): return grad_rows * factor  6.03 us
    reduce_sum x1, other arithmetic, per_device(): total = lax.psum(jnp.sum(grad_rows * grad_rows), ('dp', 'pipe'))  5.11 us
    unnamed x3, local copies, waits for them, and re-layouts  2.1 us
  transfers between devices with their start and end apart: 1, of which 1 were waited for; matrix products, arithmetic and copies ran while one was open for 2% of the time, Pallas kernels for 0%

commit v1 on v0

v1 whole, which is shorter than its diff:
```python
import functools
import math

import jax
import jax.numpy as jnp
from jax import lax
from jax.experimental import pallas as pl
from jax.experimental.pallas import tpu as pltpu
from jax.sharding import PartitionSpec as P

VOC_DEV = 1408
CHUNKS = 4
MESH = pl.DeviceIdType.MESH


def gather_kernel(n_dp, n_pipe, clip, scale, grad_ref, ids_ref, all_ref, row_ref, factor_ref,
                  held, id_held, sums, load_sem, send_sem, recv_sem, sum_send, sum_recv):
    me = lax.axis_index("dp")
    z = lax.axis_index("pipe")
    core = lax.rem(me, 2)
    to_sibling = 1 - 2 * core
    to_x = 2 - 4 * lax.rem(me // 2, 2)
    to_y = 4 - 8 * (me // 4)
    sibling, x_peer, y_peer = me + to_sibling, me + to_x, me + to_y
    diagonal = me + to_x + to_y
    relayed = me + (1 - core) * to_x + core * to_y
    relay_to = me + core * to_x + (1 - core) * to_y
    rows = held.shape[1] // CHUNKS

    load = pltpu.make_async_copy(grad_ref, held.at[me], load_sem.at[0])
    load.start()
    load_ids = pltpu.make_async_copy(ids_ref, id_held.at[me], load_sem.at[1])
    load_ids.start()

    barrier = pltpu.get_barrier_semaphore()
    for peer in (sibling, x_peer, y_peer):
        pl.semaphore_signal(barrier, inc=1, device_id=(peer, z), device_id_type=MESH)
    for step in range(1, n_pipe):
        pl.semaphore_signal(
            barrier, inc=1, device_id=(me, lax.rem(z + step, n_pipe)), device_id_type=MESH
        )
    pl.semaphore_wait(barrier, 3 + n_pipe - 1)
    load_ids.wait()
    load.wait()

    def piece(block, part):
        if part == 0:
            return id_held.at[block]
        return held.at[block, pl.ds((part - 1) * rows, rows)]

    def copy(block, part, target, kind):
        return pltpu.make_async_remote_copy(
            src_ref=piece(block, part), dst_ref=piece(block, part),
            send_sem=send_sem.at[kind, part], recv_sem=recv_sem.at[block, part],
            device_id=(target, z), device_id_type=MESH,
        )

    sent = []

    def send(block, part, target, kind):
        moving = copy(block, part, target, kind)
        moving.start()
        sent.append(moving)

    def arrived(block, part):
        copy(block, part, sibling, 0).wait_recv()

    parts = range(CHUNKS + 1)
    for part in parts:
        send(me, part, relay_to, 0)
        send(me, part, relayed, 1)
        send(me, part, sibling, 2)
    for part in parts:
        arrived(relayed, part)
        send(relayed, part, relay_to, 3)
        send(relayed, part, sibling, 4)
        arrived(relay_to, part)
        send(relay_to, part, sibling, 5)
    arrived(diagonal, 0)
    send(diagonal, 0, sibling, 6)
    for block in (sibling, sibling + to_x, sibling + to_y, sibling + to_x + to_y):
        arrived(block, 0)

    ids = jnp.concatenate([id_held[block] for block in range(n_dp)], axis=1)
    row_ref[...] = ids
    tokens = ids.shape[1]
    columns = []
    for start in range(0, tokens, 128):
        columns.append(
            jnp.broadcast_to(ids[:, start:start + 128].astype(jnp.float32), (128, 128)).T[:, :1]
        )
    column = jnp.concatenate(columns, axis=0)
    same = jnp.where(column == ids.astype(jnp.float32), 1.0, 0.0)
    here = lax.broadcasted_iota(jnp.int32, same.shape, 0)
    other = lax.broadcasted_iota(jnp.int32, same.shape, 1)
    earlier = jnp.sum(jnp.where(other < here, same, 0.0), axis=1, keepdims=True)
    first = jnp.where(earlier == 0.0, same, 0.0).astype(jnp.bfloat16)

    for part in parts[1:]:
        arrived(diagonal, part)
        send(diagonal, part, sibling, 6)
    for block in (sibling, sibling + to_x, sibling + to_y, sibling + to_x + to_y):
        for part in parts[1:]:
            arrived(block, part)

    width = held.shape[2]
    total = jnp.zeros((1, 128), jnp.float32)
    tile = 384 if width % 384 == 0 else 128
    for start in range(0, width, tile):
        block = held[:, :, start:start + tile].reshape(tokens, tile)
        summed = jnp.dot(first, block, preferred_element_type=jnp.float32)
        squares = jnp.sum(summed * summed, axis=0, keepdims=True)
        for lane in range(0, tile, 128):
            total = total + squares[:, lane:lane + 128]
    sums[z] = total
    shares = []
    for step in range(1, n_pipe):
        share = pltpu.make_async_remote_copy(
            src_ref=sums.at[z], dst_ref=sums.at[z],
            send_sem=sum_send.at[step], recv_sem=sum_recv.at[z],
            device_id=(me, lax.rem(z + step, n_pipe)), device_id_type=MESH,
        )
        share.start()
        shares.append(share)
    all_ref[...] = held[...]
    for step in range(1, n_pipe):
        origin = lax.rem(z + step, n_pipe)
        pltpu.make_async_remote_copy(
            src_ref=sums.at[origin], dst_ref=sums.at[origin],
            send_sem=sum_send.at[step], recv_sem=sum_recv.at[origin],
            device_id=(me, origin), device_id_type=MESH,
        ).wait_recv()
    whole = sums[0]
    for index in range(1, n_pipe):
        whole = whole + sums[index]
    norm = jnp.sqrt(jnp.sum(whole, axis=1, keepdims=True) * (scale * scale) + 1e-06)
    factor = jnp.minimum(1.0, clip / norm) * scale
    factor_ref[...] = jnp.broadcast_to(factor, factor_ref.shape)
    for moving in sent:
        moving.wait_send()
    for share in shares:
        share.wait_send()


def rows_kernel(ids_ref, factor_ref, all_ref, out_ref):
    height = out_ref.shape[0]
    first = lax.axis_index("dp") * VOC_DEV + pl.program_id(0) * height
    tokens = ids_ref.shape[1]
    wanted = lax.broadcasted_iota(jnp.int32, (height, tokens), 0) + first
    hot = jnp.where(wanted == ids_ref[...], 1.0, 0.0).astype(jnp.bfloat16)
    block = all_ref[...].reshape(tokens, all_ref.shape[2])
    summed = jnp.dot(hot, block, preferred_element_type=jnp.float32)
    out_ref[...] = summed * factor_ref[:, :1]


def rows_of(all_grads, ids, factor, height):
    n_dp, count, width = all_grads.shape
    tokens = n_dp * count
    return pl.pallas_call(
        rows_kernel,
        grid=(VOC_DEV // height,),
        out_shape=jax.ShapeDtypeStruct((VOC_DEV, width), jnp.float32),
        in_specs=[
            pl.BlockSpec((1, tokens), lambda i: (0, 0)),
            pl.BlockSpec((1, 128), lambda i: (0, 0)),
            pl.BlockSpec((n_dp, count, width), lambda i: (0, 0, 0)),
        ],
        out_specs=pl.BlockSpec((height, width), lambda i: (i, 0)),
        compiler_params=pltpu.CompilerParams(dimension_semantics=("arbitrary",)),
        cost_estimate=pl.CostEstimate(
            flops=2 * VOC_DEV * tokens * width, bytes_accessed=4 * VOC_DEV * width, transcendentals=0
        ),
        name="rows",
    )(ids, factor, all_grads)


def per_device(embed_grad, ids):
    n_dp, n_pipe = lax.axis_size("dp"), lax.axis_size("pipe")
    count, width = embed_grad.shape
    features = width * n_pipe
    tokens = count * n_dp
    vmem = pl.BlockSpec(memory_space=pltpu.VMEM)
    any_space = pl.BlockSpec(memory_space=pl.ANY)
    all_grads, all_ids, factor = pl.pallas_call(
        functools.partial(
            gather_kernel, n_dp, n_pipe, 0.2 * math.sqrt(tokens * features), math.sqrt(features)
        ),
        out_shape=(
            jax.ShapeDtypeStruct((n_dp, count, width), embed_grad.dtype),
            jax.ShapeDtypeStruct((1, tokens), jnp.int32),
            jax.ShapeDtypeStruct((1, 128), jnp.float32),
        ),
        in_specs=[any_space, any_space],
        out_specs=(vmem, vmem, vmem),
        scratch_shapes=[
            pltpu.VMEM((n_dp, count, width), embed_grad.dtype),
            pltpu.VMEM((n_dp, 1, count), jnp.int32),
            pltpu.VMEM((n_pipe, 1, 128), jnp.float32),
            pltpu.SemaphoreType.DMA((2,)),
            pltpu.SemaphoreType.DMA((7, CHUNKS + 1)),
            pltpu.SemaphoreType.DMA((n_dp, CHUNKS + 1)),
            pltpu.SemaphoreType.DMA((n_pipe,)),
            pltpu.SemaphoreType.DMA((n_pipe,)),
        ],
        compiler_params=pltpu.CompilerParams(collective_id=0, has_side_effects=True),
        name="gather",
    )(embed_grad, ids.reshape(1, count))
    return rows_of(all_grads, all_ids, factor, VOC_DEV // 8)


def per_device_any(embed_grad, ids):
    tokens_all = embed_grad.shape[0] * lax.axis_size("dp")
    features = embed_grad.shape[1] * lax.axis_size("pipe")
    offset = lax.axis_index("dp") * VOC_DEV
    cotangent_all = lax.all_gather(embed_grad, "dp", axis=0, tiled=True)
    local = lax.all_gather(ids, "dp", axis=0, tiled=True) - offset
    inside = (local >= 0) & (local < VOC_DEV)
    segment = jnp.where(inside, local, VOC_DEV).astype(jnp.int32)
    summed = jax.ops.segment_sum(cotangent_all.astype(jnp.float32), segment, VOC_DEV + 1)
    grad_rows = summed[:VOC_DEV] * math.sqrt(features)
    total = lax.psum(jnp.sum(grad_rows * grad_rows), ("dp", "pipe"))
    grad_norm = jnp.sqrt(total + 1e-06)
    return grad_rows * jnp.minimum(1.0, 0.2 * math.sqrt(tokens_all * features) / grad_norm)


def solution(mesh):
    placed = (P("dp", "pipe"), P("dp"))
    cube = mesh.shape["dp"] == 2 * 2 * 2
    return jax.shard_map(
        per_device if cube else per_device_any, mesh=mesh, in_specs=placed,
        out_specs=P("dp", "pipe"), check_vma=False,
    )
```

time: 104 us -> 27.2 us (0.26)
  blocking collectives: 49 us -> 0 us
  Pallas kernels: 0 us -> 27 us
  other arithmetic: 20.3 us -> 0 us
  waiting for transfers between devices: 17.1 us -> 0 us
  between operations: 14.8 us -> 0.01 us
  local copies, waits for them, and re-layouts: 2.1 us -> 0 us
    psum x1 -> x0, blocking collectives: 39.5 us -> none  [per_device(): total = lax.psum(jnp.sum(grad_rows * grad_rows), ('dp', 'pipe'))]
    pallas_call x0 -> x2, Pallas kernels: none -> 27 us  [the longest x1 20.1 us: per_device(): pl.pallas_call(functools.partial(gather_kernel, n_dp, n_pipe, 0.2 * math....]
    all_gather x1 -> x0, waiting for transfers between devices: 16.4 us -> none  [per_device(): lax.all_gather(embed_grad, 'dp', axis=0, tiled=True)]
    unnamed x1 -> x0, blocking collectives: 9.49 us -> none
    scatter-add x1 -> x0, other arithmetic: 9.15 us -> none  [segment_rows(): jax.ops.segment_sum(cotangent.astype(jnp.float32), segment, VOC_DEV + 1)]
    mul x1 -> x0, other arithmetic: 6.03 us -> none  [per_device(): return grad_rows * factor]
    reduce_sum x1 -> x0, other arithmetic: 5.11 us -> none  [per_device(): total = lax.psum(jnp.sum(grad_rows * grad_rows), ('dp', 'pipe'))]
    unnamed x3 -> x0, local copies, waits for them, and re-layouts: 2.1 us -> none
  transfers between devices with their start and end apart: 1 -> 0, of which waited for: 1 -> 0; matrix products, arithmetic and copies ran while one was open for 2% -> 0% of each run, Pallas kernels for 0% -> 0%
where the time goes in v1:
time: 27.2 us; the launch traced here: 27.1 us
  Pallas kernels  27 us (99%)
    pallas_call x1, Pallas kernels, per_device(): pl.pallas_call(functools.partial(gather_kernel, n_dp, n_pipe, 0.2 * math....  20.1 us
    pallas_call x1, Pallas kernels, rows_of(): pl.pallas_call(rows_kernel, grid=(VOC_DEV // height,), out_shape=jax.Shap...  6.92 us

profile of v1, /device:TPU:0, one launch (start us, length us, event | category | flops | bytes accessed | tf_op | source)
XLA Modules:
  0.0 27.1 jit_solution(11884416284304414971)
XLA Ops:
  0.0 20.1 %gather.1 = (bf16[8,64,1152]{2,1,0:T(8,128)(2,1)}, s32[1,512]{1,0:T(1,128)}, f32[1,128]{1,0:T(1,128)}) custom-call(bf16[64,1152]{1,0:T(8,128)(2,1)} %grad_ref.1, s32[1,64]{1,0:T(1,128)} %bitcast.1), custom_call_target="tpu_custom_call" | custom-call | tf_op jit(solution)/shard_map/gather/pallas_call | solution.py:184
  20.1 6.9 %rows.1 = f32[1408,1152]{1,0:T(8,128)} custom-call(s32[1,512]{1,0:T(1,128)} %get-tuple-element.8.ids_ref, f32[1,128]{1,0:T(1,128)} %get-tuple-element.9.factor_ref, bf16[8,64,1152]{2,1,0:T(8,128)(2,1)} %get-tuple-element.10.all_ref), custom_call_target="tpu_custom_call" | custom-call | flops 1660944384 | bytes 6488064 | tf_op jit(solution)/shard_map/rows/pallas_call | solution.py:159

commit v2 on v1

--- a/solution.py
+++ b/solution.py
@@ -10,6 +10,7 @@
 
 VOC_DEV = 1408
 CHUNKS = 4
+STRIPES = 8
 MESH = pl.DeviceIdType.MESH
 
 
@@ -142,34 +143,38 @@
         share.wait_send()
 
 
-def rows_kernel(ids_ref, factor_ref, all_ref, out_ref):
-    height = out_ref.shape[0]
-    first = lax.axis_index("dp") * VOC_DEV + pl.program_id(0) * height
+def rows_kernel(ids_ref, factor_ref, all_ref, out_ref, made, sem):
+    height = made.shape[0] // STRIPES
     tokens = ids_ref.shape[1]
-    wanted = lax.broadcasted_iota(jnp.int32, (height, tokens), 0) + first
-    hot = jnp.where(wanted == ids_ref[...], 1.0, 0.0).astype(jnp.bfloat16)
+    offset = lax.axis_index("dp") * VOC_DEV
     block = all_ref[...].reshape(tokens, all_ref.shape[2])
-    summed = jnp.dot(hot, block, preferred_element_type=jnp.float32)
-    out_ref[...] = summed * factor_ref[:, :1]
-
-
-def rows_of(all_grads, ids, factor, height):
+    factor = factor_ref[:, :1]
+    writes = []
+    for stripe in range(STRIPES):
+        where = pl.ds(stripe * height, height)
+        wanted = lax.broadcasted_iota(jnp.int32, (height, tokens), 0) + (offset + stripe * height)
+        hot = jnp.where(wanted == ids_ref[...], 1.0, 0.0).astype(jnp.bfloat16)
+        made[where] = jnp.dot(hot, block, preferred_element_type=jnp.float32) * factor
+        write = pltpu.make_async_copy(made.at[where], out_ref.at[where], sem.at[stripe])
+        write.start()
+        writes.append(write)
+    for write in writes:
+        write.wait()
+
+
+def rows_of(all_grads, ids, factor):
     n_dp, count, width = all_grads.shape
-    tokens = n_dp * count
+    vmem = pl.BlockSpec(memory_space=pltpu.VMEM)
     return pl.pallas_call(
         rows_kernel,
-        grid=(VOC_DEV // height,),
         out_shape=jax.ShapeDtypeStruct((VOC_DEV, width), jnp.float32),
-        in_specs=[
-            pl.BlockSpec((1, tokens), lambda i: (0, 0)),
-            pl.BlockSpec((1, 128), lambda i: (0, 0)),
-            pl.BlockSpec((n_dp, count, width), lambda i: (0, 0, 0)),
+        in_specs=[vmem, vmem, vmem],
+        out_specs=pl.BlockSpec(memory_space=pltpu.HBM),
+        scratch_shapes=[
+            pltpu.VMEM((VOC_DEV, width), jnp.float32),
+            pltpu.SemaphoreType.DMA((STRIPES,)),
         ],
-        out_specs=pl.BlockSpec((height, width), lambda i: (i, 0)),
-        compiler_params=pltpu.CompilerParams(dimension_semantics=("arbitrary",)),
-        cost_estimate=pl.CostEstimate(
-            flops=2 * VOC_DEV * tokens * width, bytes_accessed=4 * VOC_DEV * width, transcendentals=0
-        ),
+        compiler_params=pltpu.CompilerParams(vmem_limit_bytes=24 * 2**20),
         name="rows",
     )(ids, factor, all_grads)
 
@@ -180,17 +185,17 @@
     features = width * n_pipe
     tokens = count * n_dp
     vmem = pl.BlockSpec(memory_space=pltpu.VMEM)
-    any_space = pl.BlockSpec(memory_space=pl.ANY)
+    hbm = pl.BlockSpec(memory_space=pltpu.HBM)
     all_grads, all_ids, factor = pl.pallas_call(
         functools.partial(
             gather_kernel, n_dp, n_pipe, 0.2 * math.sqrt(tokens * features), math.sqrt(features)
         ),
         out_shape=(
-            jax.ShapeDtypeStruct((n_dp, count, width), embed_grad.dtype),
-            jax.ShapeDtypeStruct((1, tokens), jnp.int32),
-            jax.ShapeDtypeStruct((1, 128), jnp.float32),
+            pltpu.VMEM((n_dp, count, width), embed_grad.dtype),
+            pltpu.VMEM((1, tokens), jnp.int32),
+            pltpu.VMEM((1, 128), jnp.float32),
         ),
-        in_specs=[any_space, any_space],
+        in_specs=[hbm, hbm],
         out_specs=(vmem, vmem, vmem),
         scratch_shapes=[
             pltpu.VMEM((n_dp, count, width), embed_grad.dtype),
@@ -202,10 +207,12 @@
             pltpu.SemaphoreType.DMA((n_pipe,)),
             pltpu.SemaphoreType.DMA((n_pipe,)),
         ],
-        compiler_params=pltpu.CompilerParams(collective_id=0, has_side_effects=True),
+        compiler_params=pltpu.CompilerParams(
+            collective_id=0, has_side_effects=True, vmem_limit_bytes=24 * 2**20
+        ),
         name="gather",
     )(embed_grad, ids.reshape(1, count))
-    return rows_of(all_grads, all_ids, factor, VOC_DEV // 8)
+    return rows_of(all_grads, all_ids, factor)
 
 
 def per_device_any(embed_grad, ids):

time: 27.2 us -> 23.9 us (0.88)
  Pallas kernels: 27 us -> 22.2 us
  local copies, waits for them, and re-layouts: 0 us -> 1.56 us
    pallas_call x1, Pallas kernels: 6.92 us -> 3.21 us  [rows_of(): pl.pallas_call(rows_kernel, out_shape=jax.ShapeDtypeStruct((VOC_DEV, widt...]
    unnamed x0 -> x4, local copies, waits for them, and re-layouts: none -> 1.56 us
    pallas_call x1, Pallas kernels: 20.1 us -> 19 us  [per_device(): pl.pallas_call(functools.partial(gather_kernel, n_dp, n_pipe, 0.2 * math....]
where the time goes in v2:
time: 23.9 us; the launch traced here: 23.8 us
  Pallas kernels  22.2 us (93%)
  local copies, waits for them, and re-layouts  1.56 us (7%)
    pallas_call x1, Pallas kernels, per_device(): pl.pallas_call(functools.partial(gather_kernel, n_dp, n_pipe, 0.2 * math....  19 us
    pallas_call x1, Pallas kernels, rows_of(): pl.pallas_call(rows_kernel, out_shape=jax.ShapeDtypeStruct((VOC_DEV, widt...  3.21 us
    unnamed x4, local copies, waits for them, and re-layouts  1.56 us

profile of v2, /device:TPU:0, one launch (start us, length us, event | category | flops | bytes accessed | tf_op | source)
XLA Modules:
  0.0 23.8 jit_solution(3892013900256034139)
XLA Ops:
  0.0 0.0 copy-start
  0.0 0.9 %copy-done = bf16[64,1152]{1,0:T(8,128)(2,1)S(1)} copy-done((bf16[64,1152]{1,0:T(8,128)(2,1)S(1)}, bf16[64,1152]{1,0:T(8,128)(2,1)}, u32[]{:S(2)}) %copy-start) | copy-done | bytes 147480
  0.9 0.0 copy-start.1
  0.9 0.7 %copy-done.1 = s32[64]{0:T(128)S(1)} copy-done((s32[64]{0:T(128)S(1)}, s32[64]{0:T(128)}, u32[]{:S(2)}) %copy-start.1) | copy-done | bytes 280
  1.6 19.0 %gather.1 = (bf16[8,64,1152]{2,1,0:T(8,128)(2,1)S(1)}, s32[1,512]{1,0:T(1,128)S(1)}, f32[1,128]{1,0:T(1,128)S(1)}) custom-call(bf16[64,1152]{1,0:T(8,128)(2,1)S(1)} %copy-done, s32[1,64]{1,0:T(1,128)S(1)} %bitcast.1), custom_call_target="tpu_custom_call" | custom-call | tf_op jit(solution)/shard_map/gather/pallas_call | solution.py:189
  20.6 3.2 %rows.1 = f32[1408,1152]{1,0:T(8,128)} custom-call(s32[1,512]{1,0:T(1,128)S(1)} %get-tuple-element.8.ids_ref, f32[1,128]{1,0:T(1,128)S(1)} %get-tuple-element.9.factor_ref, bf16[8,64,1152]{2,1,0:T(8,128)(2,1)S(1)} %get-tuple-element.10.all_ref), custom_call_target="tpu_custom_call" | custom-call | tf_op jit(solution)/shard_map/rows/pallas_call | solution.py:168
Async XLA Ops:
  0.0 0.9 %copy-start = (bf16[64,1152]{1,0:T(8,128)(2,1)S(1)}, bf16[64,1152]{1,0:T(8,128)(2,1)}, u32[]{:S(2)}) copy-start(bf16[64,1152]{1,0:T(8,128)(2,1)} %grad_ref.1) | copy-start | bytes 442372
  0.9 0.7 %copy-start.1 = (s32[64]{0:T(128)S(1)}, s32[64]{0:T(128)}, u32[]{:S(2)}) copy-start(s32[64]{0:T(128)} %param.3) | copy-start | bytes 772

commit v3 on v2

--- a/solution.py
+++ b/solution.py
@@ -211,7 +211,10 @@
             collective_id=0, has_side_effects=True, vmem_limit_bytes=24 * 2**20
         ),
         name="gather",
-    )(embed_grad, ids.reshape(1, count))
+    )(
+        pltpu.with_memory_space_constraint(embed_grad, pltpu.HBM),
+        pltpu.with_memory_space_constraint(ids.reshape(1, count), pltpu.HBM),
+    )
     return rows_of(all_grads, all_ids, factor)
 
 

time: 23.9 us -> 22.5 us (0.941)
  local copies, waits for them, and re-layouts: 1.56 us -> 0 us
    unnamed x4 -> x0, local copies, waits for them, and re-layouts: 1.56 us -> none
where the time goes in v3:
time: 22.5 us; the launch traced here: 22.3 us
  Pallas kernels  22.3 us (99%)
    pallas_call x1, Pallas kernels, per_device(): pl.pallas_call(functools.partial(gather_kernel, n_dp, n_pipe, 0.2 * math....  19.1 us
    pallas_call x1, Pallas kernels, rows_of(): pl.pallas_call(rows_kernel, out_shape=jax.ShapeDtypeStruct((VOC_DEV, widt...  3.21 us

profile of v3, /device:TPU:0, one launch (start us, length us, event | category | flops | bytes accessed | tf_op | source)
XLA Modules:
  0.0 22.3 jit_solution(17656098229324599650)
XLA Ops:
  0.0 19.1 %gather.1 = (bf16[8,64,1152]{2,1,0:T(8,128)(2,1)S(1)}, s32[1,512]{1,0:T(1,128)S(1)}, f32[1,128]{1,0:T(1,128)S(1)}) custom-call(bf16[64,1152]{1,0:T(8,128)(2,1)} %grad_ref.1, s32[1,64]{1,0:T(1,128)} %bitcast.1), custom_call_target="tpu_custom_call" | custom-call | tf_op jit(solution)/shard_map/gather/pallas_call | solution.py:189
  19.1 3.2 %rows.1 = f32[1408,1152]{1,0:T(8,128)} custom-call(s32[1,512]{1,0:T(1,128)S(1)} %get-tuple-element.8.ids_ref, f32[1,128]{1,0:T(1,128)S(1)} %get-tuple-element.9.factor_ref, bf16[8,64,1152]{2,1,0:T(8,128)(2,1)S(1)} %get-tuple-element.10.all_ref), custom_call_target="tpu_custom_call" | custom-call | tf_op jit(solution)/shard_map/rows/pallas_call | solution.py:168
